TPU v7x, 32 devices: a whole 2x2x4 slice. The times are simulated.
32 devices in a mesh: grp: 4 (over y, x), row: 8 (over z, core).
Axes of the slice: x: 2, y: 2, z: 4, core: 2. Of those that a mesh axis runs over, the one named last changes fastest.
Arguments:
- owned_blocks: int32 [1024], P(('grp', 'row')), may hold values from 0 to 1023, as said below
- live_count: int32 [32], P(('grp', 'row')), may hold values from 9 to 36, as said below
- row_block: int32 [1152], P(('grp', 'row')), may hold values from 0 to 1023, as said below
- column_block: int32 [1152], P(('grp', 'row')), may hold values from 0 to 1023, as said below
- send_list: int32 [4, 8, 4, 24], P('grp', 'row'), may hold values from -1 to 31, as said below
- receive_list: int32 [4, 8, 4, 24], P('grp', 'row'), may hold values from -1 to 1023, as said below
- block_values: bfloat16 [1152, 256, 256], P(('grp', 'row')), as said below
- node_shift: float32 [1024, 256], P(('grp', 'row')), may hold values from 0.1 to 2
- start_vector: float32 [1024, 256], P(('grp', 'row')), as said below
Outputs:
- lanczos_basis: float32 [17, 1024, 256], P(None, ('grp', 'row'))
- tridiagonal: float32 [2, 16], replicated
Inputs may be any that keep to these rules, and one draw needn't show every extreme that they name: `owned_blocks`: A permutation of the block ids 0 to 1023. `live_count`: some device has exactly 36 live slots in every draw. `row_block`: every slot's row block is owned by the slot's device. `column_block`: every slot's column block is owned by the slot's device or appears in that device's receive_list. Nonempty entries come first in each list and are distinct; a device sends nothing to itself; send_list[p, r, g] names exactly the blocks whose ids receive_list[g, r, p] lists, in the same order. Some list is full in every draw, and some device receives a full list from every peer. `receive_list`: matches send_list as stated there. `block_values`: entries are finite and of moderate size. `start_vector`: entries are finite and of order one.
All inputs are finite; a program needn't handle non-finite values.
Results may differ from a plain program's by a relative error of at most 0.0034.
Values may be sent and summed in bfloat16 or wider, within the bound.
A program may use at most 64 MiB of HBM per device.

v0:
```python
import jax
import jax.numpy as jnp
from jax import lax
from jax.sharding import PartitionSpec as P

STEPS = 16


def shards(
    owned_blocks,
    live_count,
    row_block,
    column_block,
    send_list,
    receive_list,
    block_values,
    node_shift,
    start_vector,
):
    row_count, block_size = start_vector.shape
    slot_total = block_values.shape[0]
    groups = lax.axis_size("grp")
    entries = float(row_count * block_size * groups * lax.axis_size("row"))
    highest = lax.Precision.HIGHEST
    live_slots = jnp.arange(slot_total, dtype=jnp.int32) < live_count[0]
    known_ids = jnp.concatenate([owned_blocks, receive_list.reshape(-1)])
    column_match = column_block[:, None] == known_ids[None, :]
    column_index = jnp.argmax(column_match.astype(jnp.int32), axis=1)
    row_match = row_block[:, None] == owned_blocks[None, :]
    row_onehot = (row_match & live_slots[:, None]).astype(jnp.float32)
    ones_column = jnp.ones((block_size,), jnp.bfloat16)
    row_sums = jnp.einsum(
        "sab,b->sa", block_values, ones_column, preferred_element_type=jnp.float32
    )
    degree = jnp.dot(row_onehot.T, row_sums, precision=highest)
    diagonal = degree + node_shift
    send_index = jnp.clip(send_list[0, 0], 0, row_count - 1)

    def apply_operator(vector):
        rounded = vector.astype(jnp.bfloat16)
        outgoing = rounded[send_index]
        received = lax.all_to_all(outgoing, "grp", split_axis=0, concat_axis=0, tiled=True)
        extended = jnp.concatenate([rounded, received.reshape(-1, block_size)], axis=0)
        gathered = extended[column_index]
        products = jnp.einsum(
            "sab,sb->sa", block_values, gathered, preferred_element_type=jnp.float32
        )
        coupling = jnp.dot(row_onehot.T, products, precision=highest)
        return diagonal * vector - coupling

    start_sum = lax.psum(jnp.sum(start_vector * start_vector), ("grp", "row"))
    first_vector = start_vector * lax.rsqrt(start_sum / entries + 1e-06)
    krylov = jnp.zeros((STEPS + 1, row_count, block_size), jnp.float32).at[0].set(first_vector)
    coefficients = jnp.zeros((2, STEPS), jnp.float32)

    def lanczos_step(step_index, loop_state):
        krylov, coefficients = loop_state
        current = lax.dynamic_index_in_dim(krylov, step_index, 0, keepdims=False)
        applied = apply_operator(current)
        local_inner = jnp.einsum("kpb,pb->k", krylov, applied, precision=highest)
        inner_sum, image_sum = lax.psum((local_inner, jnp.sum(applied * applied)), ("grp", "row"))
        coefficient = inner_sum / entries
        projected = applied - jnp.einsum("k,kpb->pb", coefficient, krylov, precision=highest)
        square_mean = image_sum / entries - jnp.sum(coefficient * coefficient)
        alpha_value = lax.dynamic_index_in_dim(coefficient, step_index, 0, keepdims=False)
        coefficients = coefficients.at[0, step_index].set(alpha_value)
        coefficients = coefficients.at[1, step_index].set(jnp.sqrt(square_mean))
        next_vector = projected * lax.rsqrt(square_mean + 1e-06)
        krylov = lax.dynamic_update_index_in_dim(krylov, next_vector, step_index + 1, 0)
        return (krylov, coefficients)

    krylov, coefficients = lax.fori_loop(0, STEPS, lanczos_step, (krylov, coefficients))
    return (krylov, coefficients)


def solution(mesh):
    return jax.shard_map(
        shards,
        mesh=mesh,
        in_specs=(
            P(("grp", "row")),
            P(("grp", "row")),
            P(("grp", "row")),
            P(("grp", "row")),
            P("grp", "row", None, None),
            P("grp", "row", None, None),
            P(("grp", "row"), None, None),
            P(("grp", "row"), None),
            P(("grp", "row"), None),
        ),
        out_specs=(P(None, ("grp", "row"), None), P()),
        check_vma=False,
    )
```

profile of v0, /device:TPU:0, one launch (start us, length us, event | category | flops | bytes accessed | tf_op | source)
XLA Modules:
  0.0 1068.5 jit_solution(17623545680104668028)
XLA Ops:
  2.7 42.2 %psum.35 = f32[]{:T(128)} all-reduce(f32[]{:T(128)} %multiply_reduce_fusion.2), channel_id=1, replica_groups=mesh['grp'=4,'row'=8] {'grp','row'}, use_global_device_ids=true, to_apply=%region_1.2 | all-reduce | flops 1 | bytes 8 | tf_op jit(solution)/shard_map/psum | solution.py:51
  53.9 1013.8 %while.21 = (s32[]{:T(128)}, f32[17,32,256]{2,1,0:T(8,128)S(1)}, f32[2,16]{1,0:T(2,128)S(1)}, f32[32,256]{1,0:T(8,128)S(1)}, s32[4,24]{1,0:T(4,128)S(1)}, /*inde...) while((s32[]{:T(128)}, f32[17,32,256]{2,1,0:T(8,128)S(1)}, ...), condition=%wide.region_10.11_spmd.clone, body=%wide.region_3.10_spmd.clone.sunk | while | flops 11786108 | bytes 6645675 | solution.py:72
  59.9 4.1 all-to-all-done
  70.3 39.4 %all-reduce.3 = (f32[17]{0:T(128)S(1)}, f32[]{:T(128)}) all-reduce(f32[17]{0:T(128)S(1)} %convolution_bitcast_fusion.3, f32[]{:T(128)} %get-tuple-element.384), channel_id=1, replica_groups=mesh['grp'=4,'row'=8] {'grp','row'}, use_global_device_ids=true, to_apply=%region_4.4 | all-reduce | flops 18 | bytes 144 | tf_op jit(solution)/shard_map/while/body/eval_jaxpr/psum | solution.py:61
  123.6 4.1 all-to-all-done
  134.0 38.4 %all-reduce.3 = (f32[17]{0:T(128)S(1)}, f32[]{:T(128)}) all-reduce(f32[17]{0:T(128)S(1)} %convolution_bitcast_fusion.3, f32[]{:T(128)} %get-tuple-element.384), channel_id=1, replica_groups=mesh['grp'=4,'row'=8] {'grp','row'}, use_global_device_ids=true, to_apply=%region_4.4 | all-reduce | flops 18 | bytes 144 | tf_op jit(solution)/shard_map/while/body/eval_jaxpr/psum | solution.py:61
  181.9 3.9 all-to-all-start
  186.6 4.1 all-to-all-done
  196.9 39.3 %all-reduce.3 = (f32[17]{0:T(128)S(1)}, f32[]{:T(128)}) all-reduce(f32[17]{0:T(128)S(1)} %convolution_bitcast_fusion.3, f32[]{:T(128)} %get-tuple-element.384), channel_id=1, replica_groups=mesh['grp'=4,'row'=8] {'grp','row'}, use_global_device_ids=true, to_apply=%region_4.4 | all-reduce | flops 18 | bytes 144 | tf_op jit(solution)/shard_map/while/body/eval_jaxpr/psum | solution.py:61
  245.8 3.9 all-to-all-start
  250.4 4.1 all-to-all-done
  260.8 38.5 %all-reduce.3 = (f32[17]{0:T(128)S(1)}, f32[]{:T(128)}) all-reduce(f32[17]{0:T(128)S(1)} %convolution_bitcast_fusion.3, f32[]{:T(128)} %get-tuple-element.384), channel_id=1, replica_groups=mesh['grp'=4,'row'=8] {'grp','row'}, use_global_device_ids=true, to_apply=%region_4.4 | all-reduce | flops 18 | bytes 144 | tf_op jit(solution)/shard_map/while/body/eval_jaxpr/psum | solution.py:61
  308.7 3.9 all-to-all-start
  313.3 4.1 all-to-all-done
  323.7 39.3 %all-reduce.3 = (f32[17]{0:T(128)S(1)}, f32[]{:T(128)}) all-reduce(f32[17]{0:T(128)S(1)} %convolution_bitcast_fusion.3, f32[]{:T(128)} %get-tuple-element.384), channel_id=1, replica_groups=mesh['grp'=4,'row'=8] {'grp','row'}, use_global_device_ids=true, to_apply=%region_4.4 | all-reduce | flops 18 | bytes 144 | tf_op jit(solution)/shard_map/while/body/eval_jaxpr/psum | solution.py:61
  372.5 3.9 all-to-all-start
  377.1 4.1 all-to-all-done
  387.5 38.5 %all-reduce.3 = (f32[17]{0:T(128)S(1)}, f32[]{:T(128)}) all-reduce(f32[17]{0:T(128)S(1)} %convolution_bitcast_fusion.3, f32[]{:T(128)} %get-tuple-element.384), channel_id=1, replica_groups=mesh['grp'=4,'row'=8] {'grp','row'}, use_global_device_ids=true, to_apply=%region_4.4 | all-reduce | flops 18 | bytes 144 | tf_op jit(solution)/shard_map/while/body/eval_jaxpr/psum | solution.py:61
  435.5 3.9 all-to-all-start
  440.1 4.1 all-to-all-done
  450.5 39.3 %all-reduce.3 = (f32[17]{0:T(128)S(1)}, f32[]{:T(128)}) all-reduce(f32[17]{0:T(128)S(1)} %convolution_bitcast_fusion.3, f32[]{:T(128)} %get-tuple-element.384), channel_id=1, replica_groups=mesh['grp'=4,'row'=8] {'grp','row'}, use_global_device_ids=true, to_apply=%region_4.4 | all-reduce | flops 18 | bytes 144 | tf_op jit(solution)/shard_map/while/body/eval_jaxpr/psum | solution.py:61
  499.3 3.9 all-to-all-start
  503.9 4.1 all-to-all-done
  514.2 38.5 %all-reduce.3 = (f32[17]{0:T(128)S(1)}, f32[]{:T(128)}) all-reduce(f32[17]{0:T(128)S(1)} %convolution_bitcast_fusion.3, f32[]{:T(128)} %get-tuple-element.384), channel_id=1, replica_groups=mesh['grp'=4,'row'=8] {'grp','row'}, use_global_device_ids=true, to_apply=%region_4.4 | all-reduce | flops 18 | bytes 144 | tf_op jit(solution)/shard_map/while/body/eval_jaxpr/psum | solution.py:61
  562.2 3.9 all-to-all-start
  566.8 4.1 all-to-all-done
  577.2 39.3 %all-reduce.3 = (f32[17]{0:T(128)S(1)}, f32[]{:T(128)}) all-reduce(f32[17]{0:T(128)S(1)} %convolution_bitcast_fusion.3, f32[]{:T(128)} %get-tuple-element.384), channel_id=1, replica_groups=mesh['grp'=4,'row'=8] {'grp','row'}, use_global_device_ids=true, to_apply=%region_4.4 | all-reduce | flops 18 | bytes 144 | tf_op jit(solution)/shard_map/while/body/eval_jaxpr/psum | solution.py:61
  626.0 3.9 all-to-all-start
  630.6 4.1 all-to-all-done
  641.0 38.5 %all-reduce.3 = (f32[17]{0:T(128)S(1)}, f32[]{:T(128)}) all-reduce(f32[17]{0:T(128)S(1)} %convolution_bitcast_fusion.3, f32[]{:T(128)} %get-tuple-element.384), channel_id=1, replica_groups=mesh['grp'=4,'row'=8] {'grp','row'}, use_global_device_ids=true, to_apply=%region_4.4 | all-reduce | flops 18 | bytes 144 | tf_op jit(solution)/shard_map/while/body/eval_jaxpr/psum | solution.py:61
  689.0 3.9 all-to-all-start
  693.6 4.1 all-to-all-done
  704.0 39.3 %all-reduce.3 = (f32[17]{0:T(128)S(1)}, f32[]{:T(128)}) all-reduce(f32[17]{0:T(128)S(1)} %convolution_bitcast_fusion.3, f32[]{:T(128)} %get-tuple-element.384), channel_id=1, replica_groups=mesh['grp'=4,'row'=8] {'grp','row'}, use_global_device_ids=true, to_apply=%region_4.4 | all-reduce | flops 18 | bytes 144 | tf_op jit(solution)/shard_map/while/body/eval_jaxpr/psum | solution.py:61
  752.8 3.9 all-to-all-start
  757.4 4.1 all-to-all-done
  767.7 38.5 %all-reduce.3 = (f32[17]{0:T(128)S(1)}, f32[]{:T(128)}) all-reduce(f32[17]{0:T(128)S(1)} %convolution_bitcast_fusion.3, f32[]{:T(128)} %get-tuple-element.384), channel_id=1, replica_groups=mesh['grp'=4,'row'=8] {'grp','row'}, use_global_device_ids=true, to_apply=%region_4.4 | all-reduce | flops 18 | bytes 144 | tf_op jit(solution)/shard_map/while/body/eval_jaxpr/psum | solution.py:61
  815.7 3.9 all-to-all-start
  820.3 4.1 all-to-all-done
  830.7 39.3 %all-reduce.3 = (f32[17]{0:T(128)S(1)}, f32[]{:T(128)}) all-reduce(f32[17]{0:T(128)S(1)} %convolution_bitcast_fusion.3, f32[]{:T(128)} %get-tuple-element.384), channel_id=1, replica_groups=mesh['grp'=4,'row'=8] {'grp','row'}, use_global_device_ids=true, to_apply=%region_4.4 | all-reduce | flops 18 | bytes 144 | tf_op jit(solution)/shard_map/while/body/eval_jaxpr/psum | solution.py:61
  879.5 3.9 all-to-all-start
  884.1 4.1 all-to-all-done
  894.5 38.5 %all-reduce.3 = (f32[17]{0:T(128)S(1)}, f32[]{:T(128)}) all-reduce(f32[17]{0:T(128)S(1)} %convolution_bitcast_fusion.3, f32[]{:T(128)} %get-tuple-element.384), channel_id=1, replica_groups=mesh['grp'=4,'row'=8] {'grp','row'}, use_global_device_ids=true, to_apply=%region_4.4 | all-reduce | flops 18 | bytes 144 | tf_op jit(solution)/shard_map/while/body/eval_jaxpr/psum | solution.py:61
  942.5 3.9 all-to-all-start
  947.1 4.1 all-to-all-done
  957.4 39.3 %all-reduce.3 = (f32[17]{0:T(128)S(1)}, f32[]{:T(128)}) all-reduce(f32[17]{0:T(128)S(1)} %convolution_bitcast_fusion.3, f32[]{:T(128)} %get-tuple-element.384), channel_id=1, replica_groups=mesh['grp'=4,'row'=8] {'grp','row'}, use_global_device_ids=true, to_apply=%region_4.4 | all-reduce | flops 18 | bytes 144 | tf_op jit(solution)/shard_map/while/body/eval_jaxpr/psum | solution.py:61
  1006.3 3.9 all-to-all-start
  1010.9 4.1 all-to-all-done
  1021.2 38.5 %all-reduce.3 = (f32[17]{0:T(128)S(1)}, f32[]{:T(128)}) all-reduce(f32[17]{0:T(128)S(1)} %convolution_bitcast_fusion.3, f32[]{:T(128)} %get-tuple-element.384), channel_id=1, replica_groups=mesh['grp'=4,'row'=8] {'grp','row'}, use_global_device_ids=true, to_apply=%region_4.4 | all-reduce | flops 18 | bytes 144 | tf_op jit(solution)/shard_map/while/body/eval_jaxpr/psum | solution.py:61
  (361 shorter events, 259.8 us)
Async XLA Ops:
  0.6 53.3 %copy-start.2 = (s32[2]{0:T(128)S(1)}, s32[2]{0:T(128)}, u32[]{:S(2)}) copy-start(s32[2]{0:T(128)} %constant.226.clone.2) | copy-start | bytes 28
  0.6 52.9 %copy-start.4 = (s32[32]{0:T(128)S(1)}, s32[32]{0:T(128)}, u32[]{:S(2)}) copy-start(s32[32]{0:T(128)} %param.17) | copy-start | bytes 388
  0.7 52.9 %copy-start.5 = (s32[36]{0:T(128)S(1)}, s32[36]{0:T(128)}, u32[]{:S(2)}) copy-start(s32[36]{0:T(128)} %param.19) | copy-start | bytes 436
  0.7 52.9 %copy-start.3 = (f32[32,256]{1,0:T(8,128)S(1)}, f32[32,256]{1,0:T(8,128)}, u32[]{:S(2)}) copy-start(f32[32,256]{1,0:T(8,128)} %param.24) | copy-start | bytes 98308
  55.4 8.5 all-to-all-start
  119.0 8.6 all-to-all-start
  181.9 8.7 all-to-all-start
  245.8 8.7 all-to-all-start
  308.7 8.7 all-to-all-start
  372.5 8.7 all-to-all-start
  435.5 8.7 all-to-all-start
  499.3 8.7 all-to-all-start
  562.2 8.7 all-to-all-start
  626.0 8.7 all-to-all-start
  689.0 8.7 all-to-all-start
  752.8 8.7 all-to-all-start
  815.7 8.7 all-to-all-start
  879.5 8.7 all-to-all-start
  942.5 8.7 all-to-all-start
  1006.3 8.7 all-to-all-start
  1067.7 0.8 copy-start
  1067.7 0.8 copy-start.1
where the time goes:
time: 1070 us
  blocking collectives  665 us (62%)
  matrix products  107 us (10%)
  other arithmetic  76 us (7%)
  local copies, waits for them, and re-layouts  69 us (6%)
  waiting for transfers between devices  64.9 us (6%)
  starting transfers between devices  61.8 us (6%)
  loops' own time  22.8 us (2%)
    psum x16, blocking collectives, lanczos_step(): lax.psum((local_inner, jnp.sum(applied * applied)), ('grp', 'row'))  622 us
    all_to_all x16, waiting for transfers between devices, apply_operator(): lax.all_to_all(outgoing, 'grp', split_axis=0, concat_axis=0, tiled=True)  64.9 us
    all_to_all x16, starting transfers between devices, apply_operator(): lax.all_to_all(outgoing, 'grp', split_axis=0, concat_axis=0, tiled=True)  61.8 us
    another operation x49, other arithmetic  60.7 us
    dot_general x16, matrix products, apply_operator(): jnp.einsum('sab,sb->sa', block_values, gathered, preferred_element_type=j...  58.4 us
    psum x1, blocking collectives, shards(): start_sum = lax.psum(jnp.sum(start_vector * start_vector), ('grp', 'row'))  42.2 us
    another operation x1, loops' own time, shards(): lax.fori_loop(0, STEPS, lanczos_step, (krylov, coefficients))  22.8 us
    gather x16, local copies, waits for them, and re-layouts, apply_operator(): outgoing = rounded[send_index]  22.3 us
  transfers between devices with their start and end apart: 16, of which 16 were waited for; matrix products, arithmetic and copies ran while one was open for 1% of the time, Pallas kernels for 0%

commit v1 on v0

v1 whole, which is shorter than its diff:
```python
import functools

import jax
import jax.numpy as jnp
from jax import lax
from jax.experimental import pallas as pl
from jax.experimental.pallas import tpu as pltpu
from jax.sharding import PartitionSpec as P

STEPS = 16
LANES = 128
F32 = jnp.float32
BF16 = jnp.bfloat16
MESH = pl.DeviceIdType.MESH
NT = (((1,), (1,)), ((), ()))


def kernel(
    groups,
    ranks,
    owned_ref,
    live_ref,
    row_ref,
    column_ref,
    values_ref,
    shift_ref,
    start_ref,
    basis_ref,
    tri_ref,
    weights,
    mask,
    known,
    image,
    parts,
    ids,
    diagonal,
    weight_sem,
    image_send,
    image_recv,
    part_send,
    part_recv,
    id_send,
    id_recv,
):
    slots, block, _ = values_ref.shape
    rows = shift_ref.shape[0]
    devices = groups * ranks
    entries = float(devices * rows * block)
    my_group = lax.axis_index("grp")
    my_rank = lax.axis_index("row")
    me = my_group * ranks + my_rank
    packed_slots = -(-slots // 8) * 8

    def peer(group_step, rank_step):
        group = lax.rem(my_group + group_step, groups)
        rank = lax.rem(my_rank + rank_step, ranks)
        return group, rank

    offsets = [(g, r) for r in range(ranks - 1, -1, -1) for g in range(groups - 1, -1, -1)]
    offsets = [pair for pair in offsets if pair != (0, 0)]

    def each_other(action):
        if devices <= 64:
            for group_step, rank_step in offsets:
                action(*peer(group_step, rank_step))
        else:

            def body(at, carry):
                action(*peer(at // ranks, lax.rem(at, ranks)))
                return carry

            lax.fori_loop(1, devices, body, 0)

    weight_copy = pltpu.make_async_copy(values_ref, weights, weight_sem)
    weight_copy.start()

    barrier = pltpu.get_barrier_semaphore()
    each_other(
        lambda g, r: pl.semaphore_signal(barrier, inc=1, device_id=(g, r), device_id_type=MESH)
    )

    lane_row = lax.broadcasted_iota(jnp.int32, (1, LANES), 1)
    lane_tile = lax.broadcasted_iota(jnp.int32, (8, LANES), 1)
    wide = groups * rows
    wide_row = lax.broadcasted_iota(jnp.int32, (1, wide), 1)
    own_ids = jnp.zeros((1, wide), jnp.int32)
    own_column = jnp.zeros((rows, LANES), jnp.int32)
    row_iota = lax.broadcasted_iota(jnp.int32, (rows, LANES), 0)
    for at in range(rows):
        own_ids = jnp.where(lax.rem(wide_row, rows) == at, owned_ref[at], own_ids)
        own_column = jnp.where(row_iota == at, owned_ref[at], own_column)
    ids[0] = own_ids

    def part_sum(image_value, first):
        square = image_value * image_value
        tile = jnp.zeros((8, LANES), F32)

        def folded(product):
            total = None
            for top in range(0, rows, 8):
                for left in range(0, block, LANES):
                    piece = product[top : top + 8, left : left + LANES]
                    total = piece if total is None else total + piece
            return jnp.sum(total, axis=1, keepdims=True)

        tile = jnp.where(lane_tile == STEPS + 1, folded(square), tile)
        if not first:
            for k in range(STEPS):
                tile = jnp.where(lane_tile == k, folded(known[k, 0] * image_value), tile)
        return jnp.sum(tile, axis=0, keepdims=True)

    def image_copy(buffer, step):
        group, rank = peer(step, 0)
        return pltpu.make_async_remote_copy(
            src_ref=image.at[buffer, 0],
            dst_ref=image.at[buffer, groups - step],
            send_sem=image_send.at[buffer, step],
            recv_sem=image_recv.at[buffer, groups - step],
            device_id=(group, rank),
            device_id_type=MESH,
        )

    def image_wait(buffer, step):
        pltpu.make_async_copy(
            image.at[buffer, step], image.at[buffer, step], image_recv.at[buffer, step]
        ).wait()

    def part_start(buffer):
        def send(group, rank):
            pltpu.make_async_remote_copy(
                src_ref=parts.at[buffer, me],
                dst_ref=parts.at[buffer, me],
                send_sem=part_send.at[buffer],
                recv_sem=part_recv.at[buffer],
                device_id=(group, rank),
                device_id_type=MESH,
            ).start()

        each_other(send)

    def part_wait(buffer, sem):
        others = parts.at[buffer, pl.ds(0, devices - 1)]
        pltpu.make_async_copy(others, others, sem.at[buffer]).wait()

    def id_copy(step):
        group, rank = peer(step, 0)
        return pltpu.make_async_remote_copy(
            src_ref=ids.at[0],
            dst_ref=ids.at[groups - step],
            send_sem=id_send.at[step],
            recv_sem=id_recv.at[groups - step],
            device_id=(group, rank),
            device_id_type=MESH,
        )

    def totals(buffer):
        total = parts[buffer, 0]
        for at in range(1, devices):
            total = total + parts[buffer, at]
        total = total * (1.0 / entries)
        signed = jnp.where(lane_row <= STEPS, -total * total, 0.0)
        signed = jnp.where(lane_row == STEPS + 1, total, signed)
        square_mean = jnp.sum(signed, axis=1, keepdims=True)
        return total, square_mean

    start = start_ref[...]
    image[0, 0] = start
    parts[0, me] = part_sum(start, True)

    pl.semaphore_wait(barrier, devices - 1)
    for step in range(1, groups):
        id_copy(step).start()
    part_start(0)
    for step in range(1, groups):
        image_copy(0, step).start()

    known[...] = jnp.zeros_like(known)
    for s in range(slots):
        row = jnp.where(s < live_ref[0], row_ref[s], -1)
        mask[s] = (own_column == row).astype(F32).astype(BF16)
    column = jnp.full((packed_slots, wide), -1, jnp.int32)
    slot_iota = lax.broadcasted_iota(jnp.int32, (packed_slots, wide), 0)
    for s in range(slots):
        column = jnp.where(slot_iota == s, column_ref[s], column)

    weight_copy.wait()
    degree = jnp.zeros((rows, block), F32)
    for s in range(slots):
        lhs = jnp.concatenate([mask[s]] * (block // LANES), axis=1)
        degree = degree + lax.dot_general(lhs, weights[s], NT, preferred_element_type=F32)
    diagonal[...] = degree + shift_ref[...]

    for step in range(1, groups):
        id_copy(step).wait_send()
    for step in range(1, groups):
        pltpu.make_async_copy(ids.at[step], ids.at[step], id_recv.at[step]).wait()
    known_ids = ids[0]
    for step in range(1, groups):
        known_ids = jnp.where(wide_row // rows == step, ids[step], known_ids)
    gather = (column == known_ids).astype(F32).astype(BF16)

    def spread(total, square_mean):
        scale = jnp.broadcast_to(lax.rsqrt(square_mean + 1e-06), (8, LANES))
        tile = jnp.broadcast_to(total, (8, LANES))
        coefficients = [
            jnp.broadcast_to(tile[:, k : k + 1], (8, LANES)) for k in range(STEPS)
        ]
        return coefficients, scale

    def orthogonal(buffer, step, coefficients, scale):
        pieces = []
        for top in range(0, rows, 8):
            line = []
            for left in range(0, block, LANES):
                at = (pl.ds(top, 8), pl.ds(left, LANES))
                value = image[(buffer, step) + at]
                for k in range(STEPS):
                    value = value - coefficients[k] * known[(k, step) + at]
                line.append(value * scale)
            pieces.append(jnp.concatenate(line, axis=1))
        return jnp.concatenate(pieces, axis=0)

    def record(it, total, square_mean, alpha, beta):
        here = lane_row == it - 1
        alpha = jnp.where(here, total, alpha)
        beta = jnp.where(here, jnp.sqrt(square_mean), beta)
        return alpha, beta

    def body(it, state):
        alpha, beta = state
        now = lax.rem(it, 2)
        later = 1 - now
        part_wait(now, part_recv)
        total, square_mean = totals(now)
        alpha, beta = record(it, total, square_mean, alpha, beta)
        coefficients, scale = spread(total, square_mean)
        vectors = []
        for step in range(groups):
            if step:
                image_wait(now, step)
            vector = orthogonal(now, step, coefficients, scale)
            known[it, step] = vector
            if step == 0:
                basis_ref[it] = vector
            vectors.append(vector.astype(BF16))
        gathered = jnp.dot(
            gather, jnp.concatenate(vectors, axis=0), preferred_element_type=F32
        )
        coupling = jnp.zeros((rows, block), F32)
        for s in range(slots):
            line = jnp.broadcast_to(gathered[s : s + 1], (rows, block)).astype(BF16)
            lhs = line * jnp.concatenate([mask[s]] * (block // LANES), axis=1)
            coupling = coupling + lax.dot_general(
                lhs, weights[s], NT, preferred_element_type=F32
            )
        applied = diagonal[...] * known[it, 0] - coupling

        part_wait(now, part_send)
        for step in range(1, groups):
            image_copy(now, step).wait_send()
        image[later, 0] = applied
        parts[later, me] = part_sum(applied, False)
        part_start(later)

        @pl.when(it < STEPS - 1)
        def _():
            for step in range(1, groups):
                image_copy(later, step).start()

        return alpha, beta

    zero = jnp.zeros((1, LANES), F32)
    alpha, beta = lax.fori_loop(0, STEPS, body, (zero, zero))
    last = STEPS % 2
    part_wait(last, part_recv)
    part_wait(last, part_send)
    total, square_mean = totals(last)
    alpha, beta = record(STEPS, total, square_mean, alpha, beta)
    coefficients, scale = spread(total, square_mean)
    basis_ref[STEPS] = orthogonal(last, 0, coefficients, scale)
    tri_ref[...] = jnp.concatenate([alpha[:, :STEPS], beta[:, :STEPS]], axis=0)


def shards(
    owned_blocks,
    live_count,
    row_block,
    column_block,
    send_list,
    receive_list,
    block_values,
    node_shift,
    start_vector,
):
    rows, block = start_vector.shape
    slots = block_values.shape[0]
    groups = lax.axis_size("grp")
    ranks = lax.axis_size("row")
    devices = groups * ranks
    smem = pl.BlockSpec(memory_space=pltpu.SMEM)
    vmem = pl.BlockSpec(memory_space=pltpu.VMEM)
    dma = pltpu.SemaphoreType.DMA
    return pl.pallas_call(
        functools.partial(kernel, groups, ranks),
        out_shape=(
            jax.ShapeDtypeStruct((STEPS + 1, rows, block), F32),
            jax.ShapeDtypeStruct((2, STEPS), F32),
        ),
        in_specs=[smem, smem, smem, smem, pl.BlockSpec(memory_space=pl.ANY), vmem, vmem],
        out_specs=(vmem, vmem),
        scratch_shapes=[
            pltpu.VMEM((slots, block, block), BF16),
            pltpu.VMEM((slots, rows, LANES), BF16),
            pltpu.VMEM((STEPS, groups, rows, block), F32),
            pltpu.VMEM((2, groups, rows, block), F32),
            pltpu.VMEM((2, devices, 1, LANES), F32),
            pltpu.VMEM((groups, 1, groups * rows), jnp.int32),
            pltpu.VMEM((rows, block), F32),
            dma,
            dma((2, groups)),
            dma((2, groups)),
            dma((2,)),
            dma((2,)),
            dma((groups,)),
            dma((groups,)),
        ],
        compiler_params=pltpu.CompilerParams(
            collective_id=0, has_side_effects=True, vmem_limit_bytes=48 * 1024 * 1024
        ),
    )(owned_blocks, live_count, row_block, column_block, block_values, node_shift, start_vector)


def solution(mesh):
    return jax.shard_map(
        shards,
        mesh=mesh,
        in_specs=(
            P(("grp", "row")),
            P(("grp", "row")),
            P(("grp", "row")),
            P(("grp", "row")),
            P("grp", "row", None, None),
            P("grp", "row", None, None),
            P(("grp", "row"), None, None),
            P(("grp", "row"), None),
            P(("grp", "row"), None),
        ),
        out_specs=(P(None, ("grp", "row"), None), P()),
        check_vma=False,
    )
```

time: 1070 us -> 122 us (0.11)
  blocking collectives: 665 us -> 0 us
  Pallas kernels: 0 us -> 113 us
  matrix products: 107 us -> 0 us
  other arithmetic: 76 us -> 0 us
  waiting for transfers between devices: 64.9 us -> 0 us
  local copies, waits for them, and re-layouts: 69 us -> 7.18 us
  starting transfers between devices: 61.8 us -> 0 us
  loops' own time: 22.8 us -> 0 us
    psum x17 -> x0, blocking collectives: 665 us -> none  [the longest x16 622 us: lanczos_step(): lax.psum((local_inner, jnp.sum(applied * applied)), ('grp', 'row'))]
    pallas_call x0 -> x1, Pallas kernels: none -> 113 us  [shards(): pl.pallas_call(functools.partial(kernel, groups, ranks), out_shape=(jax.S...]
    dot_general x66 -> x0, matrix products: 107 us -> none  [the longest x16 58.4 us: apply_operator(): jnp.einsum('sab,sb->sa', block_values, gathered, preferred_element_type=j...]
    all_to_all x16 -> x0, waiting for transfers between devices: 64.9 us -> none  [apply_operator(): lax.all_to_all(outgoing, 'grp', split_axis=0, concat_axis=0, tiled=True)]
    another operation x50 -> x0, other arithmetic: 62 us -> none
    all_to_all x16 -> x0, starting transfers between devices: 61.8 us -> none  [apply_operator(): lax.all_to_all(outgoing, 'grp', split_axis=0, concat_axis=0, tiled=True)]
    gather x32 -> x0, local copies, waits for them, and re-layouts: 32.5 us -> none  [the longest x16 22.3 us: apply_operator(): outgoing = rounded[send_index]]
    scatter x33 -> x0, local copies, waits for them, and re-layouts: 24.2 us -> none  [the longest x16 12.1 us: lanczos_step(): coefficients = coefficients.at[1, step_index].set(jnp.sqrt(square_mean))]
  transfers between devices with their start and end apart: 16 -> 0, of which waited for: 16 -> 0; matrix products, arithmetic and copies ran while one was open for 1% -> 0% of each run, Pallas kernels for 0% -> 0%
where the time goes in v1:
time: 122 us
  Pallas kernels  113 us (93%)
  local copies, waits for them, and re-layouts  7.18 us (6%)
  between operations  1.3 us (1%)
    pallas_call x1, Pallas kernels, shards(): pl.pallas_call(functools.partial(kernel, groups, ranks), out_shape=(jax.S...  113 us
    unnamed x14, local copies, waits for them, and re-layouts  7.18 us

profile of v1, /device:TPU:0, one launch (start us, length us, event | category | flops | bytes accessed | tf_op | source)
XLA Modules:
  0.0 121.5 jit_solution(11688956075583664946)
XLA Ops:
  1.3 0.0 copy-start
  1.3 2.3 %copy-done = bf16[36,256,256]{2,1,0:T(8,128)(2,1)S(1)} copy-done((bf16[36,256,256]{2,1,0:T(8,128)(2,1)S(1)}, bf16[36,256,256]{2,1,0:T(8,128)(2,1)}, u32[]{:S(2)}) %copy-start) | copy-done | bytes 4718616
  3.6 0.0 copy-start.1
  3.6 0.8 copy-done.1
  4.4 0.0 copy-start.2
  4.4 0.8 copy-done.2
  5.1 0.0 copy-start.3
  5.1 0.7 copy-done.3
  5.8 0.0 copy-start.4
  5.8 0.7 copy-done.4
  6.4 0.0 copy-start.5
  6.4 0.7 copy-done.5
  7.1 113.0 %shard_map.86 = (f32[17,32,256]{2,1,0:T(8,128)S(1)}, f32[2,16]{1,0:T(2,128)S(1)}) custom-call(s32[32]{0:T(128)S(1)} %copy-done.3, s32[1]{0:T(128)S(6)} %copy.11.live_ref, s32[36]{0:T(128)S(1)} %copy-done.4, s32[36]{0:T(128)S(1)} %copy-done.5, bf16[36,256,256]{2,1,0:T(8,128)(2,1)S(1)} %copy-done, f32[32,256]{1,0:T(8,128)S(1)} %copy-done.1, ...), custom_call_target="tpu_custom_call" | custom-call | tf_op jit(solution)/shard_map/pallas_call | solution.py:303
  120.1 0.8 copy.12
  121.0 0.6 copy.13
Async XLA Ops:
  1.3 2.3 %copy-start = (bf16[36,256,256]{2,1,0:T(8,128)(2,1)S(1)}, bf16[36,256,256]{2,1,0:T(8,128)(2,1)}, u32[]{:S(2)}) copy-start(bf16[36,256,256]{2,1,0:T(8,128)(2,1)} %values_ref.1) | copy-start | bytes 14155780
  3.6 0.8 copy-start.1
  4.4 0.8 copy-start.2
  5.1 0.7 copy-start.3
  5.8 0.7 copy-start.4
  6.4 0.7 copy-start.5

commit v2 on v1

--- a/solution.py
+++ b/solution.py
@@ -13,6 +13,17 @@
 BF16 = jnp.bfloat16
 MESH = pl.DeviceIdType.MESH
 NT = (((1,), (1,)), ((), ()))
+
+
+SQUARES = STEPS + 1
+SHIFT = STEPS + 2
+
+
+def tree(terms):
+    while len(terms) > 1:
+        pairs = [terms[at] + terms[at + 1] for at in range(0, len(terms) - 1, 2)]
+        terms = pairs + terms[len(pairs) * 2 :]
+    return terms[0]
 
 
 def kernel(
@@ -30,6 +41,7 @@
     weights,
     mask,
     known,
+    mapped,
     image,
     parts,
     ids,
@@ -51,10 +63,23 @@
     me = my_group * ranks + my_rank
     packed_slots = -(-slots // 8) * 8
 
-    def peer(group_step, rank_step):
-        group = lax.rem(my_group + group_step, groups)
-        rank = lax.rem(my_rank + rank_step, ranks)
-        return group, rank
+    def wrapped(value, size):
+        return jnp.where(value >= size, value - size, value)
+
+    if devices <= 64:
+        group_at = [wrapped(my_group + step, groups) for step in range(groups)]
+        rank_at = [wrapped(my_rank + step, ranks) for step in range(ranks)]
+
+        def peer(group_step, rank_step):
+            return group_at[group_step], rank_at[rank_step]
+
+    else:
+
+        def peer(group_step, rank_step):
+            return (
+                wrapped(my_group + group_step, groups),
+                wrapped(my_rank + rank_step, ranks),
+            )
 
     offsets = [(g, r) for r in range(ranks - 1, -1, -1) for g in range(groups - 1, -1, -1)]
     offsets = [pair for pair in offsets if pair != (0, 0)]
@@ -91,22 +116,20 @@
         own_column = jnp.where(row_iota == at, owned_ref[at], own_column)
     ids[0] = own_ids
 
+    def folded(product):
+        pieces = [
+            product[top : top + 8, left : left + LANES]
+            for top in range(0, rows, 8)
+            for left in range(0, block, LANES)
+        ]
+        return jnp.sum(tree(pieces), axis=1, keepdims=True)
+
     def part_sum(image_value, first):
-        square = image_value * image_value
-        tile = jnp.zeros((8, LANES), F32)
-
-        def folded(product):
-            total = None
-            for top in range(0, rows, 8):
-                for left in range(0, block, LANES):
-                    piece = product[top : top + 8, left : left + LANES]
-                    total = piece if total is None else total + piece
-            return jnp.sum(total, axis=1, keepdims=True)
-
-        tile = jnp.where(lane_tile == STEPS + 1, folded(square), tile)
+        tile = jnp.where(lane_tile == SQUARES, folded(image_value * image_value), 0.0)
+        tile = jnp.where(lane_tile == SHIFT, folded(diagonal[...]), tile)
         if not first:
             for k in range(STEPS):
-                tile = jnp.where(lane_tile == k, folded(known[k, 0] * image_value), tile)
+                tile = jnp.where(lane_tile == k, folded(known[k] * image_value), tile)
         return jnp.sum(tile, axis=0, keepdims=True)
 
     def image_copy(buffer, step):
@@ -154,34 +177,23 @@
         )
 
     def totals(buffer):
-        total = parts[buffer, 0]
-        for at in range(1, devices):
-            total = total + parts[buffer, at]
-        total = total * (1.0 / entries)
-        signed = jnp.where(lane_row <= STEPS, -total * total, 0.0)
-        signed = jnp.where(lane_row == STEPS + 1, total, signed)
+        total = tree([parts[buffer, at] for at in range(devices)]) * (1.0 / entries)
+        signed = jnp.where(lane_row < STEPS, -total * total, 0.0)
+        signed = jnp.where(lane_row == SQUARES, total, signed)
         square_mean = jnp.sum(signed, axis=1, keepdims=True)
         return total, square_mean
 
-    start = start_ref[...]
-    image[0, 0] = start
-    parts[0, me] = part_sum(start, True)
-
-    pl.semaphore_wait(barrier, devices - 1)
-    for step in range(1, groups):
-        id_copy(step).start()
-    part_start(0)
-    for step in range(1, groups):
-        image_copy(0, step).start()
-
-    known[...] = jnp.zeros_like(known)
     for s in range(slots):
         row = jnp.where(s < live_ref[0], row_ref[s], -1)
         mask[s] = (own_column == row).astype(F32).astype(BF16)
+    known[...] = jnp.zeros_like(known)
+    mapped[...] = jnp.zeros_like(mapped)
     column = jnp.full((packed_slots, wide), -1, jnp.int32)
     slot_iota = lax.broadcasted_iota(jnp.int32, (packed_slots, wide), 0)
     for s in range(slots):
         column = jnp.where(slot_iota == s, column_ref[s], column)
+    start = start_ref[...]
+    image[0, 0] = start
 
     weight_copy.wait()
     degree = jnp.zeros((rows, block), F32)
@@ -189,6 +201,14 @@
         lhs = jnp.concatenate([mask[s]] * (block // LANES), axis=1)
         degree = degree + lax.dot_general(lhs, weights[s], NT, preferred_element_type=F32)
     diagonal[...] = degree + shift_ref[...]
+    parts[0, me] = part_sum(start, True)
+
+    pl.semaphore_wait(barrier, devices - 1)
+    for step in range(1, groups):
+        image_copy(0, step).start()
+    for step in range(1, groups):
+        id_copy(step).start()
+    part_start(0)
 
     for step in range(1, groups):
         id_copy(step).wait_send()
@@ -199,30 +219,39 @@
         known_ids = jnp.where(wide_row // rows == step, ids[step], known_ids)
     gather = (column == known_ids).astype(F32).astype(BF16)
 
-    def spread(total, square_mean):
+    def reduced(buffer):
+        part_wait(buffer, part_recv)
+        total, square_mean = totals(buffer)
+        tile = jnp.broadcast_to(total, (8, LANES))
         scale = jnp.broadcast_to(lax.rsqrt(square_mean + 1e-06), (8, LANES))
-        tile = jnp.broadcast_to(total, (8, LANES))
         coefficients = [
             jnp.broadcast_to(tile[:, k : k + 1], (8, LANES)) for k in range(STEPS)
         ]
-        return coefficients, scale
-
-    def orthogonal(buffer, step, coefficients, scale):
-        pieces = []
+        shift = jnp.broadcast_to(tile[:, SHIFT : SHIFT + 1], (8, LANES))
+        return total, square_mean, coefficients, scale, shift
+
+    def orthogonal(piece_of, history, coefficients, scale):
+        lines = []
         for top in range(0, rows, 8):
             line = []
             for left in range(0, block, LANES):
                 at = (pl.ds(top, 8), pl.ds(left, LANES))
-                value = image[(buffer, step) + at]
+                terms = [piece_of(top, left)]
                 for k in range(STEPS):
-                    value = value - coefficients[k] * known[(k, step) + at]
-                line.append(value * scale)
-            pieces.append(jnp.concatenate(line, axis=1))
-        return jnp.concatenate(pieces, axis=0)
-
-    def record(it, total, square_mean, alpha, beta):
+                    terms.append(-coefficients[k] * history[(k,) + at])
+                line.append(tree(terms) * scale)
+            lines.append(jnp.concatenate(line, axis=1))
+        return jnp.concatenate(lines, axis=0)
+
+    def vector_of(buffer, coefficients, scale):
+        def piece(top, left):
+            return image[buffer, 0, pl.ds(top, 8), pl.ds(left, LANES)]
+
+        return orthogonal(piece, known, coefficients, scale)
+
+    def record(it, total, square_mean, shift, alpha, beta):
         here = lane_row == it - 1
-        alpha = jnp.where(here, total, alpha)
+        alpha = jnp.where(here, total + shift[:1], alpha)
         beta = jnp.where(here, jnp.sqrt(square_mean), beta)
         return alpha, beta
 
@@ -230,54 +259,63 @@
         alpha, beta = state
         now = lax.rem(it, 2)
         later = 1 - now
-        part_wait(now, part_recv)
-        total, square_mean = totals(now)
-        alpha, beta = record(it, total, square_mean, alpha, beta)
-        coefficients, scale = spread(total, square_mean)
-        vectors = []
+        for step in range(1, groups):
+            image_wait(now, step)
+        high = []
+        low = []
         for step in range(groups):
-            if step:
-                image_wait(now, step)
-            vector = orthogonal(now, step, coefficients, scale)
-            known[it, step] = vector
-            if step == 0:
-                basis_ref[it] = vector
-            vectors.append(vector.astype(BF16))
-        gathered = jnp.dot(
-            gather, jnp.concatenate(vectors, axis=0), preferred_element_type=F32
+            value = image[now, step]
+            top = value.astype(BF16)
+            high.append(top)
+            low.append((value - top.astype(F32)).astype(BF16))
+        both = jnp.concatenate(
+            [jnp.concatenate(high, axis=0), jnp.concatenate(low, axis=0)], axis=1
         )
-        coupling = jnp.zeros((rows, block), F32)
+        gathered = jnp.dot(gather, both, preferred_element_type=F32)
+        product = jnp.zeros((2 * rows, block), F32)
         for s in range(slots):
-            line = jnp.broadcast_to(gathered[s : s + 1], (rows, block)).astype(BF16)
-            lhs = line * jnp.concatenate([mask[s]] * (block // LANES), axis=1)
-            coupling = coupling + lax.dot_general(
+            keep = jnp.concatenate([mask[s]] * (block // LANES), axis=1)
+            top = jnp.broadcast_to(gathered[s : s + 1, :block], (rows, block)).astype(BF16)
+            rest = jnp.broadcast_to(gathered[s : s + 1, block:], (rows, block)).astype(BF16)
+            lhs = jnp.concatenate([top * keep, rest * keep], axis=0)
+            product = product + lax.dot_general(
                 lhs, weights[s], NT, preferred_element_type=F32
             )
-        applied = diagonal[...] * known[it, 0] - coupling
-
-        part_wait(now, part_send)
+        coupling = product[:rows] + product[rows:]
+
+        total, square_mean, coefficients, scale, shift = reduced(now)
+
+        def mapped_piece(top, left):
+            at = (pl.ds(top, 8), pl.ds(left, LANES))
+            moved = (diagonal[at] - shift) * image[(now, 0) + at]
+            return moved - coupling[top : top + 8, left : left + LANES]
+
+        image_value = orthogonal(mapped_piece, mapped, coefficients, scale)
         for step in range(1, groups):
             image_copy(now, step).wait_send()
-        image[later, 0] = applied
-        parts[later, me] = part_sum(applied, False)
-        part_start(later)
+        image[later, 0] = image_value
 
         @pl.when(it < STEPS - 1)
         def _():
             for step in range(1, groups):
                 image_copy(later, step).start()
 
-        return alpha, beta
+        vector = vector_of(now, coefficients, scale)
+        known[it] = vector
+        part_wait(now, part_send)
+        parts[later, me] = part_sum(image_value, False)
+        part_start(later)
+        mapped[it] = image_value
+        basis_ref[it] = vector
+        return record(it, total, square_mean, shift, alpha, beta)
 
     zero = jnp.zeros((1, LANES), F32)
     alpha, beta = lax.fori_loop(0, STEPS, body, (zero, zero))
     last = STEPS % 2
-    part_wait(last, part_recv)
+    total, square_mean, coefficients, scale, shift = reduced(last)
     part_wait(last, part_send)
-    total, square_mean = totals(last)
-    alpha, beta = record(STEPS, total, square_mean, alpha, beta)
-    coefficients, scale = spread(total, square_mean)
-    basis_ref[STEPS] = orthogonal(last, 0, coefficients, scale)
+    alpha, beta = record(STEPS, total, square_mean, shift, alpha, beta)
+    basis_ref[STEPS] = vector_of(last, coefficients, scale)
     tri_ref[...] = jnp.concatenate([alpha[:, :STEPS], beta[:, :STEPS]], axis=0)
 
 
@@ -311,7 +349,8 @@
         scratch_shapes=[
             pltpu.VMEM((slots, block, block), BF16),
             pltpu.VMEM((slots, rows, LANES), BF16),
-            pltpu.VMEM((STEPS, groups, rows, block), F32),
+            pltpu.VMEM((STEPS, rows, block), F32),
+            pltpu.VMEM((STEPS, rows, block), F32),
             pltpu.VMEM((2, groups, rows, block), F32),
             pltpu.VMEM((2, devices, 1, LANES), F32),
             pltpu.VMEM((groups, 1, groups * rows), jnp.int32),

time: 122 us -> 107 us (0.88)
  Pallas kernels: 113 us -> 98.1 us
    pallas_call x1, Pallas kernels: 113 us -> 98.1 us  [shards(): pl.pallas_call(functools.partial(kernel, groups, ranks), out_shape=(jax.S...]
where the time goes in v2:
time: 107 us
  Pallas kernels  98.1 us (92%)
  local copies, waits for them, and re-layouts  7.18 us (7%)
  between operations  1.3 us (1%)
    pallas_call x1, Pallas kernels, shards(): pl.pallas_call(functools.partial(kernel, groups, ranks), out_shape=(jax.S...  98.1 us
    unnamed x14, local copies, waits for them, and re-layouts  7.18 us

profile of v2, /device:TPU:0, one launch (start us, length us, event | category | flops | bytes accessed | tf_op | source)
XLA Modules:
  0.0 106.5 jit_solution(2898071587827003200)
XLA Ops:
  1.3 0.0 copy-start
  1.3 2.3 %copy-done = bf16[36,256,256]{2,1,0:T(8,128)(2,1)S(1)} copy-done((bf16[36,256,256]{2,1,0:T(8,128)(2,1)S(1)}, bf16[36,256,256]{2,1,0:T(8,128)(2,1)}, u32[]{:S(2)}) %copy-start) | copy-done | bytes 4718616
  3.6 0.0 copy-start.1
  3.6 0.8 copy-done.1
  4.4 0.0 copy-start.2
  4.4 0.8 copy-done.2
  5.1 0.0 copy-start.3
  5.1 0.7 copy-done.3
  5.8 0.0 copy-start.4
  5.8 0.7 copy-done.4
  6.4 0.0 copy-start.5
  6.4 0.7 copy-done.5
  7.1 98.1 %shard_map.86 = (f32[17,32,256]{2,1,0:T(8,128)S(1)}, f32[2,16]{1,0:T(2,128)S(1)}) custom-call(s32[32]{0:T(128)S(1)} %copy-done.3, s32[1]{0:T(128)S(6)} %copy.11.live_ref, s32[36]{0:T(128)S(1)} %copy-done.4, s32[36]{0:T(128)S(1)} %copy-done.5, bf16[36,256,256]{2,1,0:T(8,128)(2,1)S(1)} %copy-done, f32[32,256]{1,0:T(8,128)S(1)} %copy-done.1, ...), custom_call_target="tpu_custom_call" | custom-call | tf_op jit(solution)/shard_map/pallas_call | solution.py:341
  105.2 0.8 copy.12
  106.0 0.6 copy.13
Async XLA Ops:
  1.3 2.3 %copy-start = (bf16[36,256,256]{2,1,0:T(8,128)(2,1)S(1)}, bf16[36,256,256]{2,1,0:T(8,128)(2,1)}, u32[]{:S(2)}) copy-start(bf16[36,256,256]{2,1,0:T(8,128)(2,1)} %values_ref.1) | copy-start | bytes 14155780
  3.6 0.8 copy-start.1
  4.4 0.8 copy-start.2
  5.1 0.7 copy-start.3
  5.8 0.7 copy-start.4
  6.4 0.7 copy-start.5

commit v3 on v2

--- a/solution.py
+++ b/solution.py
@@ -12,7 +12,6 @@
 F32 = jnp.float32
 BF16 = jnp.bfloat16
 MESH = pl.DeviceIdType.MESH
-NT = (((1,), (1,)), ((), ()))
 
 
 SQUARES = STEPS + 1
@@ -196,10 +195,16 @@
     image[0, 0] = start
 
     weight_copy.wait()
+
+    def flip(s, carry):
+        weights[s] = weights[s].T
+        return carry
+
+    lax.fori_loop(0, slots, flip, 0)
     degree = jnp.zeros((rows, block), F32)
     for s in range(slots):
         lhs = jnp.concatenate([mask[s]] * (block // LANES), axis=1)
-        degree = degree + lax.dot_general(lhs, weights[s], NT, preferred_element_type=F32)
+        degree = degree + jnp.dot(lhs, weights[s], preferred_element_type=F32)
     diagonal[...] = degree + shift_ref[...]
     parts[0, me] = part_sum(start, True)
 
@@ -278,9 +283,7 @@
             top = jnp.broadcast_to(gathered[s : s + 1, :block], (rows, block)).astype(BF16)
             rest = jnp.broadcast_to(gathered[s : s + 1, block:], (rows, block)).astype(BF16)
             lhs = jnp.concatenate([top * keep, rest * keep], axis=0)
-            product = product + lax.dot_general(
-                lhs, weights[s], NT, preferred_element_type=F32
-            )
+            product = product + jnp.dot(lhs, weights[s], preferred_element_type=F32)
         coupling = product[:rows] + product[rows:]
 
         total, square_mean, coefficients, scale, shift = reduced(now)

time: 107 us -> 101 us (0.944)
  Pallas kernels: 98.1 us -> 92.5 us
    pallas_call x1, Pallas kernels: 98.1 us -> 92.5 us  [shards(): pl.pallas_call(functools.partial(kernel, groups, ranks), out_shape=(jax.S...]
where the time goes in v3:
time: 101 us
  Pallas kernels  92.5 us (92%)
  local copies, waits for them, and re-layouts  7.18 us (7%)
  between operations  1.3 us (1%)
    pallas_call x1, Pallas kernels, shards(): pl.pallas_call(functools.partial(kernel, groups, ranks), out_shape=(jax.S...  92.5 us
    unnamed x14, local copies, waits for them, and re-layouts  7.18 us

profile of v3, /device:TPU:0, one launch (start us, length us, event | category | flops | bytes accessed | tf_op | source)
XLA Modules:
  0.0 101.0 jit_solution(12977934178527826960)
XLA Ops:
  1.3 0.0 copy-start
  1.3 2.3 %copy-done = bf16[36,256,256]{2,1,0:T(8,128)(2,1)S(1)} copy-done((bf16[36,256,256]{2,1,0:T(8,128)(2,1)S(1)}, bf16[36,256,256]{2,1,0:T(8,128)(2,1)}, u32[]{:S(2)}) %copy-start) | copy-done | bytes 4718616
  3.6 0.0 copy-start.1
  3.6 0.8 copy-done.1
  4.4 0.0 copy-start.2
  4.4 0.8 copy-done.2
  5.1 0.0 copy-start.3
  5.1 0.7 copy-done.3
  5.8 0.0 copy-start.4
  5.8 0.7 copy-done.4
  6.4 0.0 copy-start.5
  6.4 0.7 copy-done.5
  7.1 92.5 %shard_map.86 = (f32[17,32,256]{2,1,0:T(8,128)S(1)}, f32[2,16]{1,0:T(2,128)S(1)}) custom-call(s32[32]{0:T(128)S(1)} %copy-done.3, s32[1]{0:T(128)S(6)} %copy.11.live_ref, s32[36]{0:T(128)S(1)} %copy-done.4, s32[36]{0:T(128)S(1)} %copy-done.5, bf16[36,256,256]{2,1,0:T(8,128)(2,1)S(1)} %copy-done, f32[32,256]{1,0:T(8,128)S(1)} %copy-done.1, ...), custom_call_target="tpu_custom_call" | custom-call | tf_op jit(solution)/shard_map/pallas_call | solution.py:344
  99.6 0.8 copy.12
  100.5 0.6 copy.13
Async XLA Ops:
  1.3 2.3 %copy-start = (bf16[36,256,256]{2,1,0:T(8,128)(2,1)S(1)}, bf16[36,256,256]{2,1,0:T(8,128)(2,1)}, u32[]{:S(2)}) copy-start(bf16[36,256,256]{2,1,0:T(8,128)(2,1)} %values_ref.1) | copy-start | bytes 14155780
  3.6 0.8 copy-start.1
  4.4 0.8 copy-start.2
  5.1 0.7 copy-start.3
  5.8 0.7 copy-start.4
  6.4 0.7 copy-start.5
